TPU v7x, 32 devices: a whole 2x2x4 slice. The times are simulated.
32 devices in a mesh: path: 4 (over z), tm: 8 (over y, x, core).
Axes of the slice: x: 2, y: 2, z: 4, core: 2. Of those that a mesh axis runs over, the one named last changes fastest.
Arguments:
- values: bfloat16 [2048, 16, 2048], P('path', 'tm'), may hold values from -5 to 5
- hazard: float32 [16, 2048], P('tm', 'path'), may hold values from 0.0125 to 0.1875
- spread: float32 [16], P('tm'), may hold values from 0.3 to 3
- trade_set: int32 [2048], replicated, may hold values from 0 to 255
Outputs:
- pathwise_fva: float32 [2048, 256], P(('path', 'tm'))
- set_fva: float32 [256], P(('path', 'tm'))
All inputs are finite; a program needn't handle non-finite values.
Results may differ from a plain program's by a relative error of at most 0.0003.
Values sent between devices are 32-bit elements; how exact they have to be, the bound alone decides.
A program may use at most 64 MiB of HBM per device.

v0:
```python
import jax
import jax.numpy as jnp
from jax import lax
from jax.sharding import PartitionSpec as P

SETS = 256


def on_device(values, hazard, spread, trade_set):
    paths_dev, dates_dev, trades = values.shape
    dates_total = dates_dev * lax.axis_size("tm")
    paths_total = paths_dev * lax.axis_size("path")
    onehot = (trade_set[:, None] == jnp.arange(SETS, dtype=jnp.int32)[None, :]).astype(jnp.bfloat16)
    netted = jnp.dot(
        values.reshape(paths_dev * dates_dev, trades), onehot, preferred_element_type=jnp.float32
    )
    positive = jnp.maximum(netted.reshape(paths_dev, dates_dev, SETS), 0.0)
    survival = jnp.exp(-jnp.cumsum(hazard, axis=0))
    block_product = survival[-1]
    weights = jnp.transpose(spread[:, None] * survival)
    local_sum = jnp.einsum("pt,pts->ps", weights, positive, precision=lax.Precision.HIGHEST)
    gathered_sums, gathered_products = (
        lax.all_to_all(local_sum[None], "tm", split_axis=1, concat_axis=0, tiled=True),
        lax.all_to_all(block_product[None], "tm", split_axis=1, concat_axis=0, tiled=True),
    )
    earlier = jnp.concatenate(
        [jnp.ones_like(gathered_products[:1]), jnp.cumprod(gathered_products[:-1], axis=0)], axis=0
    )
    shares = jnp.einsum("kp,kps->ps", earlier, gathered_sums, precision=lax.Precision.HIGHEST)
    pathwise_fva = shares / dates_total
    set_part = jnp.sum(pathwise_fva, axis=0) / paths_total
    set_fva = lax.psum_scatter(set_part, ("path", "tm"), scatter_dimension=0, tiled=True)
    return (pathwise_fva, set_fva)


def solution(mesh):
    in_specs = (P("path", "tm", None), P("tm", "path"), P("tm"), P())
    out_specs = (P(("path", "tm"), None), P(("path", "tm")))
    return jax.shard_map(
        on_device, mesh=mesh, in_specs=in_specs, out_specs=out_specs, check_vma=False
    )
```

profile of v0, /device:TPU:0, one launch (start us, length us, event | category | flops | bytes accessed | tf_op | source)
XLA Modules:
  0.0 80.7 jit_solution(11877485971977223632)
XLA Ops:
  0.6 0.7 reduce_window_sum.11
  1.3 0.7 multiply_bitcast_fusion
  2.1 0.7 all_to_all.9
  2.8 5.2 %all-to-all-start = ((f32[1,8,64]{2,0,1:T(1,128)}), f32[1,8,64]{2,0,1:T(1,128)S(1)}, u32[]{:S(2)}, u32[]{:S(2)}) async-start(f32[1,8,64]{2,0,1:T(1,128)} %all_to_all.9), calls=%async_computation | async-start | bytes 8192 | tf_op jit(solution)/shard_map/all_to_all | solution.py:24
  8.0 0.1 copy.8
  8.1 0.0 copy-start
  8.1 7.2 %reshape.21 = bf16[1024,2048]{1,0:T(8,128)(2,1)} reshape(bf16[512,2,2048]{2,1,0:T(2,128)(2,1)} %param.4) | data formatting | bytes 8388608 | tf_op jit(solution)/shard_map/reshape | solution.py:15
  15.4 0.0 copy-done
  15.4 3.8 %fusion.1 = f32[1024,256]{0,1:T(8,128)S(1)} fusion(bf16[1024,2048]{1,0:T(8,128)(2,1)} %reshape.21, s32[2048]{0:T(1024)S(1)} %copy-done), kind=kOutput, calls=%fused_computation.3 | convolution fusion | flops 1075052544 | bytes 5251072 | tf_op jit(solution)/shard_map/dot_general | solution.py:14
  19.2 0.3 copy.7
  19.6 0.6 max.15
  20.2 3.8 %fusion.7 = f32[512,1,256]{2,1,0:T(1,128)S(1)} fusion(f32[512,2,1]{1,2,0:T(1,128)S(1)} %copy.8, f32[512,2,256]{2,1,0:T(2,128)S(1)} %max.15), kind=kOutput, calls=%fused_computation.16 | convolution fusion | flops 3145728 | bytes 1576960 | tf_op jit(solution)/shard_map/pt,pts->ps/dot_general | solution.py:21
  24.1 1.1 %broadcast_in_dim.2 = f32[1,512,256]{2,0,1:T(1,128)} reshape(f32[512,256]{1,0:T(8,128)S(1)} %bitcast.23) | data formatting | bytes 1048576 | tf_op jit(solution)/shard_map/broadcast_in_dim | solution.py:23
  25.2 0.0 all-to-all-done
  25.2 4.2 %all-to-all-start.1 = ((f32[1,512,256]{2,0,1:T(1,128)}), f32[1,512,256]{2,0,1:T(1,128)S(1)}, u32[]{:S(2)}, u32[]{:S(2)}) async-start(f32[1,512,256]{2,0,1:T(1,128)} %broadcast_in_dim.2), calls=%async_computation.1 | async-start | bytes 1048576 | tf_op jit(solution)/shard_map/all_to_all | solution.py:23
  29.5 0.1 copy.10
  29.6 9.6 %all-to-all-done.1 = f32[1,512,256]{2,0,1:T(1,128)S(1)} async-done(((f32[1,512,256]{2,0,1:T(1,128)}), f32[1,512,256]{2,0,1:T(1,128)S(1)}, u32[]{:S(2)}, u32[]{:S(2)}) %all-to-all-start.1) | async-done | bytes 524320 | tf_op jit(solution)/shard_map/all_to_all | solution.py:23
  39.2 0.9 %fusion.4 = f32[64,1,256]{2,1,0:T(1,128)S(1)} fusion(f32[8,64,1]{0,2,1:T(1,128)S(1)} %copy.10, f32[8,64,256]{2,1,0:T(8,128)S(1)} %bitcast.22), kind=kOutput, calls=%fused_computation.5 | convolution fusion | flops 1572864 | bytes 591872 | tf_op jit(solution)/shard_map/kp,kps->ps/dot_general | solution.py:29
  40.0 0.6 fusion.6
  40.7 39.4 %all-reduce.1 = f32[256]{0:T(256)S(1)} all-reduce(f32[256]{0:T(256)S(1)} %broadcast_multiply_fusion), channel_id=2, replica_groups=mesh['path'=4,'tm'=8] {'path','tm'}, use_global_device_ids=true, to_apply=%region_3.4.clone | all-reduce | flops 256 | bytes 2048
  80.1 0.6 dynamic-slice
  (8 shorter events, 0.1 us)
Async XLA Ops:
  2.8 22.5 %all-to-all-start = ((f32[1,8,64]{2,0,1:T(1,128)}), f32[1,8,64]{2,0,1:T(1,128)S(1)}, u32[]{:S(2)}, u32[]{:S(2)}) async-start(f32[1,8,64]{2,0,1:T(1,128)} %all_to_all.9), calls=%async_computation | async-start | bytes 8192 | tf_op jit(solution)/shard_map/all_to_all | solution.py:24
  8.1 7.2 %copy-start = (s32[2048]{0:T(1024)S(1)}, s32[2048]{0:T(1024)}, u32[]{:S(2)}) copy-start(s32[2048]{0:T(1024)} %param.7) | copy-start | bytes 24580
  25.2 13.9 %all-to-all-start.1 = ((f32[1,512,256]{2,0,1:T(1,128)}), f32[1,512,256]{2,0,1:T(1,128)S(1)}, u32[]{:S(2)}, u32[]{:S(2)}) async-start(f32[1,512,256]{2,0,1:T(1,128)} %broadcast_in_dim.2), calls=%async_computation.1 | async-start | bytes 1048576 | tf_op jit(solution)/shard_map/all_to_all | solution.py:23
where the time goes:
time: 81.2 us; the launch traced here: 80.7 us
  blocking collectives  39.4 us (49%)
  local copies, waits for them, and re-layouts  10.9 us (13%)
  waiting for transfers between devices  9.58 us (12%)
  starting transfers between devices  9.4 us (12%)
  matrix products  8.55 us (11%)
  other arithmetic  2.11 us (3%)
    unnamed x1, blocking collectives  39.4 us
    all_to_all x1, waiting for transfers between devices, on_device(): lax.all_to_all(local_sum[None], 'tm', split_axis=1, concat_axis=0, tiled=...  9.57 us
    reshape x1, local copies, waits for them, and re-layouts, on_device(): values.reshape(paths_dev * dates_dev, trades)  7.22 us
    all_to_all x1, starting transfers between devices, on_device(): lax.all_to_all(block_product[None], 'tm', split_axis=1, concat_axis=0, ti...  5.2 us
    all_to_all x1, starting transfers between devices, on_device(): lax.all_to_all(local_sum[None], 'tm', split_axis=1, concat_axis=0, tiled=...  4.2 us
    dot_general x1, matrix products, on_device(): jnp.dot(values.reshape(paths_dev * dates_dev, trades), onehot, preferred_...  3.85 us
    dot_general x1, matrix products, on_device(): jnp.einsum('pt,pts->ps', weights, positive, precision=lax.Precision.HIGHEST)  3.85 us
  transfers between devices with their start and end apart: 2, of which 1 were waited for; matrix products, arithmetic and copies ran while one was open for 21% of the time, Pallas kernels for 0%

commit v1 on v0

--- a/solution.py
+++ b/solution.py
@@ -21,7 +21,15 @@
     local_sum = jnp.einsum("pt,pts->ps", weights, positive, precision=lax.Precision.HIGHEST)
     gathered_sums, gathered_products = (
         lax.all_to_all(local_sum[None], "tm", split_axis=1, concat_axis=0, tiled=True),
-        lax.all_to_all(block_product[None], "tm", split_axis=1, concat_axis=0, tiled=True),
+        jnp.concatenate(
+            lax.all_to_all(
+                jnp.stack(jnp.split(block_product[None], lax.axis_size("tm"), axis=1), axis=0),
+                axis_name="tm",
+                split_axis=0,
+                concat_axis=0,
+            ),
+            axis=0,
+        ),
     )
     earlier = jnp.concatenate(
         [jnp.ones_like(gathered_products[:1]), jnp.cumprod(gathered_products[:-1], axis=0)], axis=0

time: 81.2 us -> 84.9 us (1.046)
  local copies, waits for them, and re-layouts: 10.9 us -> 14.6 us
    unnamed x5 -> x12, local copies, waits for them, and re-layouts: 0.63 us -> 4.42 us
where the time goes in v1:
time: 84.9 us; the launch traced here: 84.3 us
  blocking collectives  39.4 us (46%)
  local copies, waits for them, and re-layouts  14.6 us (17%)
  waiting for transfers between devices  9.58 us (11%)
  starting transfers between devices  9.38 us (11%)
  matrix products  8.57 us (10%)
  other arithmetic  2.11 us (2%)
    unnamed x1, blocking collectives  39.4 us
    all_to_all x1, waiting for transfers between devices, on_device(): lax.all_to_all(local_sum[None], 'tm', split_axis=1, concat_axis=0, tiled=...  9.57 us
    reshape x1, local copies, waits for them, and re-layouts, on_device(): values.reshape(paths_dev * dates_dev, trades)  7.22 us
    all_to_all x1, starting transfers between devices, on_device(): lax.all_to_all(jnp.stack(jnp.split(block_product[None], lax.axis_size('tm...  5.2 us
    unnamed x12, local copies, waits for them, and re-layouts  4.42 us
    all_to_all x1, starting transfers between devices, on_device(): lax.all_to_all(local_sum[None], 'tm', split_axis=1, concat_axis=0, tiled=...  4.18 us
    dot_general x1, matrix products, on_device(): jnp.dot(values.reshape(paths_dev * dates_dev, trades), onehot, preferred_...  3.87 us
    dot_general x1, matrix products, on_device(): jnp.einsum('pt,pts->ps', weights, positive, precision=lax.Precision.HIGHEST)  3.85 us
  transfers between devices with their start and end apart: 2, of which 1 were waited for; matrix products, arithmetic and copies ran while one was open for 21% of the time, Pallas kernels for 0%

profile of v1, /device:TPU:0, one launch (start us, length us, event | category | flops | bytes accessed | tf_op | source)
XLA Modules:
  0.0 84.3 jit_solution(13043413894317564552)
XLA Ops:
  0.6 0.7 reduce_window_sum.11
  1.3 0.7 multiply_bitcast_fusion
  2.1 0.5 constant_dynamic-update-slice_fusion.7
  2.6 0.6 constant_dynamic-update-slice_fusion.6
  3.2 0.5 constant_dynamic-update-slice_fusion.5
  3.7 0.6 constant_dynamic-update-slice_fusion.4
  4.3 0.5 constant_dynamic-update-slice_fusion.3
  4.8 0.6 constant_dynamic-update-slice_fusion.2
  5.4 0.5 constant_dynamic-update-slice_fusion.1
  5.9 0.6 constant_dynamic-update-slice_fusion
  6.4 5.2 %all-to-all-start = ((f32[8,1,64]{2,1,0:T(1,128)}), f32[8,1,64]{2,1,0:T(1,128)S(1)}, u32[]{:S(2)}, u32[]{:S(2)}) async-start(f32[8,1,64]{2,1,0:T(1,128)} %constant_dynamic-update-slice_fusion), calls=%async_computation | async-start | bytes 8192 | tf_op jit(solution)/shard_map/all_to_all | solution.py:25
  11.6 0.1 copy.8
  11.8 7.2 %reshape.17 = bf16[1024,2048]{1,0:T(8,128)(2,1)} reshape(bf16[512,2,2048]{2,1,0:T(2,128)(2,1)} %param.4) | data formatting | bytes 8388608 | tf_op jit(solution)/shard_map/reshape | solution.py:15
  19.0 3.9 %fusion.1 = f32[1024,256]{0,1:T(8,128)S(1)} fusion(bf16[1024,2048]{1,0:T(8,128)(2,1)} %reshape.17, s32[2048]{0:T(1024)S(1)} %copy-done), kind=kOutput, calls=%fused_computation.3 | convolution fusion | flops 1075052544 | bytes 5251072 | tf_op jit(solution)/shard_map/dot_general | solution.py:14
  22.9 0.3 copy.7
  23.2 0.6 max.15
  23.9 3.8 %fusion.7 = f32[512,1,256]{2,1,0:T(1,128)S(1)} fusion(f32[512,2,1]{1,2,0:T(1,128)S(1)} %copy.8, f32[512,2,256]{2,1,0:T(2,128)S(1)} %max.15), kind=kOutput, calls=%fused_computation.31 | convolution fusion | flops 3145728 | bytes 1576960 | tf_op jit(solution)/shard_map/pt,pts->ps/dot_general | solution.py:21
  27.8 1.1 %broadcast_in_dim.2 = f32[1,512,256]{2,0,1:T(1,128)} reshape(f32[512,256]{1,0:T(8,128)S(1)} %bitcast.55) | data formatting | bytes 1048576 | tf_op jit(solution)/shard_map/broadcast_in_dim | solution.py:23
  28.9 4.2 %all-to-all-start.1 = ((f32[1,512,256]{2,0,1:T(1,128)}), f32[1,512,256]{2,0,1:T(1,128)S(1)}, u32[]{:S(2)}, u32[]{:S(2)}) async-start(f32[1,512,256]{2,0,1:T(1,128)} %broadcast_in_dim.2), calls=%async_computation.1 | async-start | bytes 1048576 | tf_op jit(solution)/shard_map/all_to_all | solution.py:23
  33.2 9.6 %all-to-all-done.1 = f32[1,512,256]{2,0,1:T(1,128)S(1)} async-done(((f32[1,512,256]{2,0,1:T(1,128)}), f32[1,512,256]{2,0,1:T(1,128)S(1)}, u32[]{:S(2)}, u32[]{:S(2)}) %all-to-all-start.1) | async-done | bytes 524320 | tf_op jit(solution)/shard_map/all_to_all | solution.py:23
  42.9 0.9 %fusion.4 = f32[64,1,256]{2,1,0:T(1,128)S(1)} fusion(f32[8,64,1]{0,2,1:T(1,128)S(1)} %copy.10, f32[8,64,256]{2,1,0:T(8,128)S(1)} %bitcast.54), kind=kOutput, calls=%fused_computation.5 | convolution fusion | flops 1572864 | bytes 591872 | tf_op jit(solution)/shard_map/kp,kps->ps/dot_general | solution.py:37
  43.7 0.6 fusion.6
  44.4 39.4 %all-reduce.1 = f32[256]{0:T(256)S(1)} all-reduce(f32[256]{0:T(256)S(1)} %broadcast_multiply_fusion), channel_id=2, replica_groups=mesh['path'=4,'tm'=8] {'path','tm'}, use_global_device_ids=true, to_apply=%region_3.4.clone | all-reduce | flops 256 | bytes 2048
  83.8 0.6 dynamic-slice
  (11 shorter events, 0.2 us)
Async XLA Ops:
  6.4 22.5 %all-to-all-start = ((f32[8,1,64]{2,1,0:T(1,128)}), f32[8,1,64]{2,1,0:T(1,128)S(1)}, u32[]{:S(2)}, u32[]{:S(2)}) async-start(f32[8,1,64]{2,1,0:T(1,128)} %constant_dynamic-update-slice_fusion), calls=%async_computation | async-start | bytes 8192 | tf_op jit(solution)/shard_map/all_to_all | solution.py:25
  11.8 7.2 %copy-start = (s32[2048]{0:T(1024)S(1)}, s32[2048]{0:T(1024)}, u32[]{:S(2)}) copy-start(s32[2048]{0:T(1024)} %param.7) | copy-start | bytes 24580
  28.9 13.9 %all-to-all-start.1 = ((f32[1,512,256]{2,0,1:T(1,128)}), f32[1,512,256]{2,0,1:T(1,128)S(1)}, u32[]{:S(2)}, u32[]{:S(2)}) async-start(f32[1,512,256]{2,0,1:T(1,128)} %broadcast_in_dim.2), calls=%async_computation.1 | async-start | bytes 1048576 | tf_op jit(solution)/shard_map/all_to_all | solution.py:23
